TPU v7x, 32 devices: a whole 2x2x4 slice. The times are simulated.
32 devices in a mesh: gx: 8 (over z, x), gy: 4 (over y, core).
Axes of the slice: x: 2, y: 2, z: 4, core: 2. Of those that a mesh axis runs over, the one named last changes fastest.
Arguments:
- vectors: float32 [8, 2, 2, 128, 1024], P(None, None, None, 'gx', 'gy'), may hold values from -6 to 6
- bonds: float32 [3, 128, 1024], P(None, 'gx', 'gy'), may hold values from 0.5 to 1.5
- onsite: float32 [2, 128, 1024], P(None, 'gx', 'gy'), may hold values from -1 to 1
Outputs:
- moment_rows: float32 [2, 3, 3, 128], P(None, None, None, 'gx')
- left_last: bfloat16 [8, 2, 2, 128, 1024], P(None, None, None, 'gx', 'gy')
- right_last: bfloat16 [8, 2, 2, 128, 1024], P(None, None, None, 'gx', 'gy')
All inputs are finite; a program needn't handle non-finite values.
Results may differ from a plain program's by a relative error of at most 0.001.
Values sent between devices are 32-bit elements; how exact they have to be, the bound alone decides.
A program may use at most 64 MiB of HBM per device.

v0:
```python
import functools
import jax
import jax.numpy as jnp
from jax import lax
from jax.experimental import pallas as pl
from jax.experimental.pallas import tpu as pltpu
from jax.sharding import PartitionSpec as P

MOMENTS = 3
SCALE = 6.0
EDGE = 2
GROUP = 4
HALF = 64
LANES = 128
GRANT = 16 * 1024 * 1024
MESH = pl.DeviceIdType.MESH


def bond_terms(a, b, fields, left, right, up, down):
    b0, b1, b2, b1d, b2r = fields
    return b0 * b, b1 * up(b) + b2 * left(b), b0 * a, b1d * down(a) + b2r * right(a)


def kernel(
    gxn, gyn, vec, bonds, onsite, out_mom, lbuf, rbuf,
    x, f, fd, g, c_own, c_left, c_right, halo_f, halo_x, keep, acc, part_mom,
    load_sem, send_sem, recv_sem, msend_sem, mrecv_sem,
):
    vectors, _, _, rows, cols = vec.shape
    tall = x.shape[3]
    tiles = cols // LANES
    last = rows - EDGE
    gx = lax.axis_index("gx")
    gy = lax.axis_index("gy")

    def peer(dx, dy):
        return (lax.rem(gx + dx + gxn, gxn), lax.rem(gy + dy + gyn, gyn))

    barrier = pltpu.get_barrier_semaphore()
    near = [(dx % gxn, dy % gyn) for dx in (-1, 0, 1) for dy in (-1, 0, 1)]
    near += [(0, dy) for dy in range(gyn)]
    near = sorted(set(near) - {(0, 0)})
    for dx, dy in near:
        pl.semaphore_signal(barrier, inc=1, device_id=peer(dx, dy), device_id_type=MESH)

    loads = [
        pltpu.make_async_copy(vec, x.at[:, :, :, 0:rows, :], load_sem.at[0]),
        pltpu.make_async_copy(bonds, f.at[0:3, 0:rows, :], load_sem.at[1]),
        pltpu.make_async_copy(onsite, f.at[3:5, 0:rows, :], load_sem.at[2]),
    ]
    for copy in loads:
        copy.start()
    sends = []

    def send(src, dst, dx, dy):
        n = len(sends)
        copy = pltpu.make_async_remote_copy(
            src_ref=src, dst_ref=dst, send_sem=send_sem.at[n], recv_sem=recv_sem.at[n],
            device_id=peer(dx, dy), device_id_type=MESH,
        )
        copy.start()
        sends.append(copy)

    for copy in loads:
        copy.wait()

    acc[...] = jnp.zeros_like(acc)
    pl.semaphore_wait(barrier, len(near))

    core = slice(0, rows)
    send(x.at[:, :, 0, 0:2, :], x.at[:, :, 0, rows : rows + 2, :], -1, 0)
    send(x.at[:, :, 1, rows - 2 : rows, :], x.at[:, :, 1, tall - 2 : tall, :], 1, 0)
    send(x.at[:, :, 1, 0:1, :], x.at[:, :, 1, rows : rows + 1, :], -1, 0)
    send(x.at[:, :, 0, rows - 1 : rows, :], x.at[:, :, 0, tall - 1 : tall, :], 1, 0)
    send(f.at[:, 0:2, :], f.at[:, rows : rows + 2, :], -1, 0)
    send(f.at[:, rows - 2 : rows, :], f.at[:, tall - 2 : tall, :], 1, 0)

    lane = lax.broadcasted_iota(jnp.int32, (rows, LANES), 1)
    spot = lax.rem(lane, HALF)

    def packed(items):
        total = jnp.zeros((rows, LANES), jnp.float32)
        for k, (first, final) in enumerate(items):
            both = jnp.where(lane < HALF, first, final)
            moved = pltpu.roll(both, GROUP * k + EDGE, 1)
            total = jnp.where(spot // GROUP == k, moved, total) if k else moved
        total = jnp.where(lane < HALF, total, pltpu.roll(total, HALF, 1))
        return total

    def edges(ref, *index):
        return ref[(*index, slice(0, rows), slice(0, LANES))], ref[
            (*index, slice(0, rows), slice(cols - LANES, cols))
        ]

    for sub in range(2):
        c_own[sub, 0:rows] = packed(
            [edges(x, v, p, sub) for v in range(vectors) for p in range(2)]
        )
    c_own[2, 0:rows] = packed([edges(f, k) for k in range(5)])

    send(c_own.at[:, core, :], c_right.at[:, core, :], 0, -1)
    send(c_own.at[:, core, :], c_left.at[:, core, :], 0, 1)
    top, bottom = c_own.at[:, 0:EDGE, :], c_own.at[:, last:rows, :]
    past, ahead = slice(rows, rows + EDGE), slice(tall - EDGE, tall)
    send(top, c_own.at[:, past, :], -1, 0)
    send(top, c_right.at[:, past, :], -1, -1)
    send(top, c_left.at[:, past, :], -1, 1)
    send(bottom, c_own.at[:, ahead, :], 1, 0)
    send(bottom, c_right.at[:, ahead, :], 1, -1)
    send(bottom, c_left.at[:, ahead, :], 1, 1)

    def scaled(i, t, item):
        g[0, i, :, tile(t)] = item * (1.0 / SCALE)
        g[1, i, :, tile(t)] = item * (2.0 / SCALE)
        if i < 5:
            g[2, i, :, tile(t)] = item * ((-1.0 if i else 2.0) / (SCALE * SCALE))

    def tile(t):
        return slice(t * LANES, (t + 1) * LANES)

    for copy in sends[4:6]:
        copy.wait_recv()
    for t in range(tiles):
        fd[0, :, tile(t)] = pltpu.roll(f[1, :, tile(t)], tall - 1, 0)
        for i, item in ((0, f[0, :, tile(t)]), (1, f[1, :, tile(t)]), (2, f[2, :, tile(t)]),
                        (3, fd[0, :, tile(t)]), (5, f[3, :, tile(t)]), (6, f[4, :, tile(t)])):
            scaled(i, t, item)
    for copy in sends[:4] + sends[6:]:
        copy.wait_recv()

    tlane = lax.broadcasted_iota(jnp.int32, (tall, LANES), 1)
    tspot = lax.rem(tlane, GROUP)
    from_left = (tlane < HALF) & (tspot < EDGE)
    from_right = (tlane >= HALF) & (tspot >= EDGE)

    def joined(k):
        return jnp.where(
            from_left, c_left[k], jnp.where(from_right, c_right[k], c_own[k])
        )

    def up(t):
        return pltpu.roll(t, 1, 0)

    def down(t):
        return pltpu.roll(t, t.shape[0] - 1, 0)

    field_tile = joined(2)
    tgroup = lax.rem(tlane, HALF)
    for k in range(5):
        t = pltpu.roll(field_tile, LANES - GROUP * k, 1) if k else field_tile
        t = jnp.where(tgroup < GROUP, t, 0.0)
        step = GROUP
        while step < HALF:
            t = t + pltpu.roll(t, step, 1)
            step *= 2
        halo_f[k] = t
    halo_f[5] = down(halo_f[1])
    halo_f[6] = pltpu.roll(halo_f[2], LANES - 1, 1)

    lane_last = tlane == LANES - 1
    lane_first = tlane == 0

    def tile(t):
        return slice(t * LANES, (t + 1) * LANES)

    after = pltpu.roll(halo_f[2], LANES - 1 - (HALF + EDGE), 1)
    for t in reversed(range(tiles)):
        turned = pltpu.roll(f[2, :, tile(t)], LANES - 1, 1)
        fd[1, :, tile(t)] = jnp.where(lane_last, after, turned)
        after = turned

    sixth = 1.0 / SCALE
    half_square = 0.5 * SCALE * SCALE
    for t in range(tiles):
        scaled(4, t, fd[1, :, tile(t)])

    def h_fields(width=tall):
        return tuple(halo_f[k] for k in (0, 1, 2, 5, 6))

    h_on = (halo_f[3], halo_f[4])

    def h_terms(a, b):
        return bond_terms(
            a, b, h_fields(), lambda t: pltpu.roll(t, 1, 1),
            lambda t: pltpu.roll(t, LANES - 1, 1), up, down,
        )

    def energy(a, b, terms, on, factor):
        a0, a12, b0, b12 = terms
        return (on[0] * a + (a0 + a12)) * factor, (on[1] * b + (b0 + b12)) * factor

    def speed(terms):
        a0, a12, b0, b12 = terms
        return a0 - 0.5 * a12, 0.5 * b12 - b0

    q0 = (joined(0), joined(1))
    t0 = h_terms(*q0)
    q1 = energy(*q0, t0, h_on, 1.0)
    m0 = speed(t0)
    h1 = energy(*q1, h_terms(*q1), h_on, 1.0)
    q2 = (h1[0] - half_square * q0[0], h1[1] - half_square * q0[1])
    m1 = energy(*m0, h_terms(*m0), h_on, sixth)
    for k, pair in enumerate((q0, q1, q2, m0, m1)):
        halo_x[k, 0], halo_x[k, 1] = pair

    short = slice(0, rows)

    def one_vector(v, carry):
        for part in range(2):
            turn_b = lax.rem(2 * LANES - (GROUP * (2 * v + part) + 1), LANES)
            turn_a = lax.rem(3 * LANES - 1 - (HALF + GROUP * (2 * v + part) + EDGE), LANES)

            def terms(pair, k, cut, w=None):
                a, b = pair
                rim_b = pltpu.roll(halo_x[k, 1], turn_b, 1)
                rim_a = pltpu.roll(halo_x[k, 0], turn_a, 1)
                keep_rows = (lambda t: t[0:rows]) if cut else (lambda t: t)
                first, final = keep_rows(lane_first), keep_rows(lane_last)
                size = short if cut else slice(0, tall)
                b_turn = [pltpu.roll(keep_rows(t), 1, 1) for t in b]
                a_turn = [pltpu.roll(keep_rows(t), LANES - 1, 1) for t in a]
                found = []
                for t in range(tiles):
                    prev = keep_rows(rim_b) if t == 0 else b_turn[t - 1]
                    nxt = keep_rows(rim_a) if t == tiles - 1 else a_turn[t + 1]
                    left = jnp.where(first, prev, b_turn[t])
                    right = jnp.where(final, nxt, a_turn[t])
                    if w is None:
                        f0, f1, f2 = (f[i, size, tile(t)] for i in range(3))
                        d1, d2 = fd[0, size, tile(t)], fd[1, size, tile(t)]
                    else:
                        f0, f1, f2, d1, d2 = (g[w, i, size, tile(t)] for i in range(5))
                    a0 = f0 * keep_rows(b[t])
                    a12 = f1 * keep_rows(up(b[t])) + f2 * left
                    b0 = f0 * keep_rows(a[t])
                    b12 = d1 * keep_rows(down(a[t])) + d2 * right
                    found.append((a0, a12, b0, b12))
                return found

            def stepped(pair, found, cut, w=None, minus=None, times=None):
                a_new, b_new = [], []
                size = short if cut else slice(0, tall)
                for t in range(tiles):
                    if w is None:
                        on = (f[3, size, tile(t)], f[4, size, tile(t)])
                    else:
                        on = (g[w, 5, size, tile(t)], g[w, 6, size, tile(t)])
                    a0, a12, b0, b12 = found[t]
                    a = on[0] * pair[0][t][size] + (a0 + a12)
                    b = on[1] * pair[1][t][size] + (b0 + b12)
                    if minus is not None:
                        less = [minus[i][t][size] for i in range(2)]
                        if times is not None:
                            less = [item * times for item in less]
                        a, b = a - less[0], b - less[1]
                    a_new.append(a)
                    b_new.append(b)
                return a_new, b_new

            def moved(found):
                both = [speed(item) for item in found]
                return [item[0] for item in both], [item[1] for item in both]

            def store(slot, pair):
                for sub in range(2):
                    for t in range(tiles):
                        keep[slot, part, sub, :, tile(t)] = pair[sub][t][0:rows]

            q0 = tuple([x[v, part, sub, :, tile(t)] for t in range(tiles)] for sub in range(2))
            t0 = terms(q0, 0, False)
            m0 = moved(t0)
            store(0, m0)
            q1 = stepped(q0, t0, False)
            t1 = terms(q1, 1, False)
            store(3, moved(t1))
            q2 = stepped(q1, t1, False, None, q0, half_square)
            n2 = [[], []]
            for a0, a12, b0, b12 in terms(q2, 2, True, 2):
                n2[0].append(a0 + a12)
                n2[1].append(-(b0 + b12))
            store(4, n2)
            m1 = stepped(m0, terms(m0, 3, False, 0), False, 0)
            store(1, m1)
            m2 = stepped(m1, terms(m1, 4, True, 1), True, 1, m0)
            store(2, m2)
            for sub in range(2):
                for t in range(tiles):
                    for buf, pair in ((lbuf, m2), (rbuf, n2)):
                        value = pair[sub][t]
                        value = -value if part == 0 else value
                        buf[v, 1 - part, sub, :, tile(t)] = value.astype(jnp.bfloat16)

        for r in range(0, rows, 8):
            band = slice(r, r + 8)
            sums = [[[acc[p, n, m, band, :] for m in range(MOMENTS)] for n in range(MOMENTS)] for p in range(2)]
            for sub in range(2):
                for t in range(tiles):
                    at = [[keep[s, p, sub, band, tile(t)] for p in range(2)] for s in range(5)]
                    for n in range(MOMENTS):
                        for m in range(MOMENTS):
                            left = at[n]
                            right = at[0] if m == 0 else at[2 + m]
                            sums[0][n][m] = sums[0][n][m] + (left[0] * right[0] + left[1] * right[1])
                            sums[1][n][m] = sums[1][n][m] + (left[0] * right[1] - left[1] * right[0])
            for p in range(2):
                for n in range(MOMENTS):
                    for m in range(MOMENTS):
                        acc[p, n, m, band, :] = sums[p][n][m]
        return carry

    lax.fori_loop(0, vectors, one_vector, 0)

    for p in range(2):
        for n in range(MOMENTS):
            acc[p, n, 1] = acc[p, n, 1] * sixth
    count = 2 * MOMENTS * MOMENTS * rows
    part_mom[0] = lax.dot_general(
        jnp.ones((8, LANES), jnp.float32), acc[...].reshape(count, LANES),
        (((1,), (1,)), ((), ())), precision=lax.Precision.HIGHEST,
        preferred_element_type=jnp.float32,
    )
    swaps = []
    for d in range(1, gyn):
        copy = pltpu.make_async_remote_copy(
            src_ref=part_mom.at[0, 0:1], dst_ref=part_mom.at[d, 0:1],
            send_sem=msend_sem.at[d - 1], recv_sem=mrecv_sem.at[d - 1],
            device_id=peer(0, d), device_id_type=MESH,
        )
        copy.start()
        swaps.append(copy)
    for copy in swaps:
        copy.wait_recv()
    total = part_mom[0]
    for d in range(1, gyn):
        total = total + part_mom[d]
    out_mom[...] = total / float(vectors * cols * gyn)
    for copy in sends + swaps:
        copy.wait_send()


def writer(total, lbuf, rbuf, out_mom, out_left, out_right, out_sem):
    outs = [
        pltpu.make_async_copy(lbuf, out_left, out_sem.at[0]),
        pltpu.make_async_copy(rbuf, out_right, out_sem.at[1]),
    ]
    for copy in outs:
        copy.start()
    rows = out_mom.shape[3]
    for p in range(2):
        for n in range(MOMENTS):
            for m in range(MOMENTS):
                k = (p * MOMENTS + n) * MOMENTS + m
                out_mom[n, m, p : p + 1, :] = total[0:1, k * rows : (k + 1) * rows]
    for copy in outs:
        copy.wait()


def solution(mesh):
    gxn, gyn = mesh.shape["gx"], mesh.shape["gy"]

    def per_device(vectors, bonds, onsite):
        count, _, _, rows, cols = vectors.shape
        tall = rows + 8
        f32 = jnp.float32
        in_hbm = pl.BlockSpec(memory_space=pltpu.HBM)
        last = jax.ShapeDtypeStruct(vectors.shape, jnp.bfloat16)
        sends = 16
        in_vmem = pl.BlockSpec(memory_space=pltpu.VMEM)
        sums = (8, 2 * MOMENTS * MOMENTS * rows)
        made = pl.pallas_call(
            functools.partial(kernel, gxn, gyn),
            out_shape=(
                pltpu.VMEM(sums, f32),
                pltpu.VMEM(vectors.shape, jnp.bfloat16),
                pltpu.VMEM(vectors.shape, jnp.bfloat16),
            ),
            in_specs=[in_hbm] * 3,
            out_specs=(in_vmem,) * 3,
            scratch_shapes=[
                pltpu.VMEM((count, 2, 2, tall, cols), f32),
                pltpu.VMEM((5, tall, cols), f32),
                pltpu.VMEM((2, tall, cols), f32),
                pltpu.VMEM((3, 7, tall, cols), f32),
                pltpu.VMEM((3, tall, LANES), f32),
                pltpu.VMEM((3, tall, LANES), f32),
                pltpu.VMEM((3, tall, LANES), f32),
                pltpu.VMEM((7, tall, LANES), f32),
                pltpu.VMEM((5, 2, tall, LANES), f32),
                pltpu.VMEM((5, 2, 2, rows, cols), f32),
                pltpu.VMEM((2, MOMENTS, MOMENTS, rows, LANES), f32),
                pltpu.VMEM((gyn, *sums), f32),
                pltpu.SemaphoreType.DMA((3,)),
                pltpu.SemaphoreType.DMA((sends,)),
                pltpu.SemaphoreType.DMA((sends,)),
                pltpu.SemaphoreType.DMA((gyn - 1,)),
                pltpu.SemaphoreType.DMA((gyn - 1,)),
            ],
            compiler_params=pltpu.CompilerParams(
                collective_id=0, has_side_effects=True, vmem_limit_bytes=GRANT
            ),
        )(*(pltpu.with_memory_space_constraint(array, pltpu.HBM) for array in (vectors, bonds, onsite)))
        made = [pltpu.with_memory_space_constraint(array, pltpu.VMEM) for array in made]
        moments, left, right = pl.pallas_call(
            writer,
            out_shape=(
                jax.ShapeDtypeStruct((MOMENTS, MOMENTS, 2, rows), f32), last, last,
            ),
            in_specs=[in_vmem] * 3,
            out_specs=(in_vmem, in_hbm, in_hbm),
            scratch_shapes=[pltpu.SemaphoreType.DMA((2,))],
            compiler_params=pltpu.CompilerParams(vmem_limit_bytes=GRANT),
        )(*made)
        return jnp.transpose(moments, (2, 0, 1, 3)), left, right

    return jax.shard_map(
        per_device,
        mesh=mesh,
        in_specs=(P(None, None, None, "gx", "gy"), P(None, "gx", "gy"), P(None, "gx", "gy")),
        out_specs=(
            P(None, None, None, "gx"),
            P(None, None, None, "gx", "gy"),
            P(None, None, None, "gx", "gy"),
        ),
        check_vma=False,
    )
```

profile of v0, /device:TPU:0, one launch (start us, length us, event | category | flops | bytes accessed | tf_op | source)
XLA Modules:
  0.0 18.8 jit_solution(15524659747923477126)
XLA Ops:
  0.6 16.8 %shard_map.58 = (f32[8,288]{1,0:T(8,128)S(1)}, bf16[8,2,2,16,256]{4,3,2,1,0:T(8,128)(2,1)S(1)}, bf16[8,2,2,16,256]{4,3,2,1,0:T(8,128)(2,1)S(1)}) custom-call(f32[8,2,2,16,256]{4,3,2,1,0:T(8,128)} %vec.1, f32[3,16,256]{2,1,0:T(8,128)} %bonds.1, f32[2,16,256]{2,1,0:T(8,128)} %onsite.1), custom_call_target="tpu_custom_call" | custom-call | tf_op jit(solution)/shard_map/pallas_call | solution.py:370
  17.4 1.4 %shard_map.59 = (f32[3,3,2,16]{3,2,1,0:T(2,128)}, bf16[8,2,2,16,256]{4,3,2,1,0:T(8,128)(2,1)}, bf16[8,2,2,16,256]{4,3,2,1,0:T(8,128)(2,1)}) custom-call(f32[8,288]{1,0:T(8,128)S(1)} %get-tuple-element.9.total, bf16[8,2,2,16,256]{4,3,2,1,0:T(8,128)(2,1)S(1)} %get-tuple-element.10.lbuf, bf16[8,2,2,16,256]{4,3,2,1,0:T(8,128)(2,1)S(1)} %get-tuple-element.11.rbuf), custom_call_target="tpu_custom_call" | custom-call | tf_op jit(solution)/shard_map/pallas_call | solution.py:403
where the time goes:
time: 19 us; the launch traced here: 18.8 us
  Pallas kernels  18.2 us (96%)
  between operations  0.64 us (3%)
    pallas_call x1, Pallas kernels, per_device(): pl.pallas_call(functools.partial(kernel, gxn, gyn), out_shape=(pltpu.VMEM...  16.8 us
    pallas_call x1, Pallas kernels, per_device(): pl.pallas_call(writer, out_shape=(jax.ShapeDtypeStruct((MOMENTS, MOMENTS,...  1.41 us

commit v1 on v0

--- a/solution.py
+++ b/solution.py
@@ -36,13 +36,6 @@
     def peer(dx, dy):
         return (lax.rem(gx + dx + gxn, gxn), lax.rem(gy + dy + gyn, gyn))
 
-    barrier = pltpu.get_barrier_semaphore()
-    near = [(dx % gxn, dy % gyn) for dx in (-1, 0, 1) for dy in (-1, 0, 1)]
-    near += [(0, dy) for dy in range(gyn)]
-    near = sorted(set(near) - {(0, 0)})
-    for dx, dy in near:
-        pl.semaphore_signal(barrier, inc=1, device_id=peer(dx, dy), device_id_type=MESH)
-
     loads = [
         pltpu.make_async_copy(vec, x.at[:, :, :, 0:rows, :], load_sem.at[0]),
         pltpu.make_async_copy(bonds, f.at[0:3, 0:rows, :], load_sem.at[1]),
@@ -50,6 +43,13 @@
     ]
     for copy in loads:
         copy.start()
+    barrier = pltpu.get_barrier_semaphore()
+    near = [(dx % gxn, dy % gyn) for dx in (-1, 0, 1) for dy in (-1, 0, 1)]
+    near += [(0, dy) for dy in range(gyn)]
+    near = sorted(set(near) - {(0, 0)})
+    for dx, dy in near:
+        pl.semaphore_signal(barrier, inc=1, device_id=peer(dx, dy), device_id_type=MESH)
+
     sends = []
 
     def send(src, dst, dx, dy):
@@ -338,19 +338,21 @@
         copy.wait_send()
 
 
-def writer(total, lbuf, rbuf, out_mom, out_left, out_right, out_sem):
+def writer(total, lbuf, rbuf, out_mom, out_left, out_right, mom, out_sem):
     outs = [
         pltpu.make_async_copy(lbuf, out_left, out_sem.at[0]),
         pltpu.make_async_copy(rbuf, out_right, out_sem.at[1]),
     ]
     for copy in outs:
         copy.start()
-    rows = out_mom.shape[3]
+    rows = mom.shape[3]
     for p in range(2):
         for n in range(MOMENTS):
             for m in range(MOMENTS):
                 k = (p * MOMENTS + n) * MOMENTS + m
-                out_mom[n, m, p : p + 1, :] = total[0:1, k * rows : (k + 1) * rows]
+                mom[n, m, p : p + 1, :] = total[0:1, k * rows : (k + 1) * rows]
+    outs.append(pltpu.make_async_copy(mom, out_mom, out_sem.at[2]))
+    outs[2].start()
     for copy in outs:
         copy.wait()
 
@@ -406,8 +408,11 @@
                 jax.ShapeDtypeStruct((MOMENTS, MOMENTS, 2, rows), f32), last, last,
             ),
             in_specs=[in_vmem] * 3,
-            out_specs=(in_vmem, in_hbm, in_hbm),
-            scratch_shapes=[pltpu.SemaphoreType.DMA((2,))],
+            out_specs=(in_hbm,) * 3,
+            scratch_shapes=[
+                pltpu.VMEM((MOMENTS, MOMENTS, 2, rows), f32),
+                pltpu.SemaphoreType.DMA((3,)),
+            ],
             compiler_params=pltpu.CompilerParams(vmem_limit_bytes=GRANT),
         )(*made)
         return jnp.transpose(moments, (2, 0, 1, 3)), left, right

time: 19 us -> 18.4 us (0.968)
  Pallas kernels: 18.2 us -> 17.6 us
    pallas_call x1, Pallas kernels: 1.41 us -> 0.82 us  [per_device(): pl.pallas_call(writer, out_shape=(jax.ShapeDtypeStruct((MOMENTS, MOMENTS,...]
where the time goes in v1:
time: 18.4 us; the launch traced here: 18.2 us
  Pallas kernels  17.6 us (96%)
  between operations  0.64 us (3%)
    pallas_call x1, Pallas kernels, per_device(): pl.pallas_call(functools.partial(kernel, gxn, gyn), out_shape=(pltpu.VMEM...  16.8 us
    pallas_call x1, Pallas kernels, per_device(): pl.pallas_call(writer, out_shape=(jax.ShapeDtypeStruct((MOMENTS, MOMENTS,...  0.82 us

profile of v1, /device:TPU:0, one launch (start us, length us, event | category | flops | bytes accessed | tf_op | source)
XLA Modules:
  0.0 18.2 jit_solution(5196785077276209818)
XLA Ops:
  0.6 16.8 %shard_map.58 = (f32[8,288]{1,0:T(8,128)S(1)}, bf16[8,2,2,16,256]{4,3,2,1,0:T(8,128)(2,1)S(1)}, bf16[8,2,2,16,256]{4,3,2,1,0:T(8,128)(2,1)S(1)}) custom-call(f32[8,2,2,16,256]{4,3,2,1,0:T(8,128)} %vec.1, f32[3,16,256]{2,1,0:T(8,128)} %bonds.1, f32[2,16,256]{2,1,0:T(8,128)} %onsite.1), custom_call_target="tpu_custom_call" | custom-call | tf_op jit(solution)/shard_map/pallas_call | solution.py:372
  17.4 0.8 %shard_map.59 = (f32[3,3,2,16]{3,2,1,0:T(2,128)}, bf16[8,2,2,16,256]{4,3,2,1,0:T(8,128)(2,1)}, bf16[8,2,2,16,256]{4,3,2,1,0:T(8,128)(2,1)}) custom-call(f32[8,288]{1,0:T(8,128)S(1)} %get-tuple-element.9.total, bf16[8,2,2,16,256]{4,3,2,1,0:T(8,128)(2,1)S(1)} %get-tuple-element.10.lbuf, bf16[8,2,2,16,256]{4,3,2,1,0:T(8,128)(2,1)S(1)} %get-tuple-element.11.rbuf), custom_call_target="tpu_custom_call" | custom-call | tf_op jit(solution)/shard_map/pallas_call | solution.py:405

commit v2 on v1

v2 whole, which is shorter than its diff:
```python
import functools
import jax
import jax.numpy as jnp
from jax import lax
from jax.experimental import pallas as pl
from jax.experimental.pallas import tpu as pltpu
from jax.sharding import PartitionSpec as P

MOMENTS = 3
SCALE = 6.0
EDGE = 2
GROUP = 8
HALF = 64
LANES = 128
SUBS = 8
SLOTS = 5
UNROLL = 8
GRANT = 32 * 1024 * 1024
MESH = pl.DeviceIdType.MESH
SIXTH = 1.0 / SCALE
HALF_SQUARE = 0.5 * SCALE * SCALE
BENT_INNER = (2.0, -1.0, -1.0, -1.0, -1.0)
BENT_WINDOW = (2.0, -1.0, -1.0, 2.0, -1.0)


def tile(t):
    return slice(t * LANES, (t + 1) * LANES)


def up(t):
    return pltpu.roll(t, 1, 0)


def down(t):
    return pltpu.roll(t, t.shape[0] - 1, 0)


def speed(terms):
    a0, a12, b0, b12 = terms
    return a0 - 0.5 * a12, 0.5 * b12 - b0


def energy(pair, terms, on, factor=None):
    a0, a12, b0, b12 = terms
    a, b = on[0] * pair[0] + (a0 + a12), on[1] * pair[1] + (b0 + b12)
    return (a, b) if factor is None else (a * factor, b * factor)


def add_products(sums, left, right):
    for n in range(MOMENTS):
        for m in range(MOMENTS):
            (p, q), (r, s) = left[n], right[m]
            sums[0][n][m] = sums[0][n][m] + (p * r + q * s)
            sums[1][n][m] = sums[1][n][m] + (p * s - q * r)


def rights_of(at):
    return [at[0], at[3], at[4]]


def masked(mask, at):
    return [[jnp.where(mask, item, 0.0) for item in at[n]] for n in range(MOMENTS)]


def each_sum():
    return [(p, n, m) for p in range(2) for n in range(MOMENTS) for m in range(MOMENTS)]


def kernel(
    gxn, gyn, vec, bonds, onsite, out_mom, lbuf, rbuf,
    x, xe, f, fw, fo, hw, gb, gw, cc, c_own, c_left, c_right, hf, cv, bw, lk, keep, acc, acw, part_mom,
    load_sem, send_sem, recv_sem, msend_sem, mrecv_sem,
):
    vectors, _, _, rows, cols = vec.shape
    tall = c_own.shape[1]
    tiles = cols // LANES
    last = tiles - 1
    gx = lax.axis_index("gx")
    gy = lax.axis_index("gy")

    def peer(dx, dy):
        return (lax.rem(gx + dx + gxn, gxn), lax.rem(gy + dy + gyn, gyn))

    low, high = slice(0, EDGE), slice(SUBS - EDGE, SUBS)
    loads = [
        pltpu.make_async_copy(vec.at[:, :, :, 0:EDGE, :], xe.at[:, :, :, low, :], load_sem.at[0]),
        pltpu.make_async_copy(
            vec.at[:, :, :, rows - EDGE : rows, :], xe.at[:, :, :, high, :], load_sem.at[1]
        ),
        pltpu.make_async_copy(bonds, f.at[0:3], load_sem.at[2]),
        pltpu.make_async_copy(onsite, f.at[3:5], load_sem.at[3]),
        pltpu.make_async_copy(vec, x, load_sem.at[4]),
    ]
    for copy in loads:
        copy.start()

    barrier = pltpu.get_barrier_semaphore()
    near = [(0, dy) for dy in range(gyn)]
    near += [(dx % gxn, dy % gyn) for dx in (-1, 1) for dy in (-1, 0, 1)]
    near = [one for k, one in enumerate(near) if one != (0, 0) and one not in near[:k]]
    for dx, dy in near:
        pl.semaphore_signal(barrier, inc=1, device_id=peer(dx, dy), device_id_type=MESH)

    hw[:, :, 0, 1 : SUBS - EDGE, :] = jnp.zeros((vectors, 2, SUBS - EDGE - 1, cols), jnp.float32)
    hw[:, :, 1, EDGE : SUBS - 1, :] = jnp.zeros((vectors, 2, SUBS - EDGE - 1, cols), jnp.float32)
    acc[...] = jnp.zeros_like(acc)
    sends = []

    def send(src, dst, dx, dy):
        n = len(sends)
        copy = pltpu.make_async_remote_copy(
            src_ref=src, dst_ref=dst, send_sem=send_sem.at[n], recv_sem=recv_sem.at[n],
            device_id=peer(dx, dy), device_id_type=MESH,
        )
        copy.start()
        sends.append(copy)

    def packed(items):
        count = items[0][0].shape[0]
        lane = lax.broadcasted_iota(jnp.int32, (count, LANES), 1)
        spot = lax.rem(lane, HALF)
        total = None
        for k, (first, final) in enumerate(items):
            both = jnp.where(lane < HALF, first, final)
            moved = pltpu.roll(both, GROUP * k + GROUP // 2, 1)
            total = jnp.where(spot // GROUP == k, moved, total) if k else moved
        return jnp.where(lane < HALF, total, pltpu.roll(total, HALF, 1))

    def ends(ref, *index):
        return ref[(*index, slice(None), slice(0, LANES))], ref[
            (*index, slice(None), slice(cols - LANES, cols))
        ]

    sub8 = lax.broadcasted_iota(jnp.int32, (SUBS, LANES), 0)
    lane8 = lax.broadcasted_iota(jnp.int32, (SUBS, LANES), 1)

    def window_a(t):
        return jnp.where(
            sub8 < 4, pltpu.roll(t[0:SUBS], 1, 0), pltpu.roll(t[rows - SUBS : rows], SUBS - 2, 0)
        )

    def window_b(t):
        return jnp.where(
            sub8 < 4, pltpu.roll(t[0:SUBS], 2, 0), pltpu.roll(t[rows - SUBS : rows], SUBS - 1, 0)
        )

    for copy in loads[:4]:
        copy.wait()
    for p in range(2):
        for sub in range(2):
            cc[2 * p + sub] = packed([ends(xe, v, p, sub) for v in range(vectors)])

    def rim_rows(t):
        return jnp.where(sub8 < 4, t[0:SUBS], t[rows - SUBS : rows])

    cc[4] = packed([tuple(rim_rows(t) for t in ends(f, k)) for k in range(5)])
    pl.semaphore_wait(barrier, len(near))

    send(f.at[0:4, 0:2, :], fw.at[0:4, SUBS - 2 : SUBS, :], -1, 0)
    send(f.at[4:5, 0:1, :], fw.at[4:5, SUBS - 1 : SUBS, :], -1, 0)
    send(f.at[0:4, rows - 1 : rows, :], fw.at[0:4, 0:1, :], 1, 0)
    send(f.at[4:5, rows - 2 : rows, :], fw.at[4:5, 0:2, :], 1, 0)
    past, ahead = slice(rows, rows + EDGE), slice(tall - EDGE, tall)
    for dst, dy in ((c_right, -1), (c_left, 1), (c_own, 0)):
        send(cc.at[:, low, :], dst.at[:, past, :], -1, dy)
        send(cc.at[:, high, :], dst.at[:, ahead, :], 1, dy)
    send(xe.at[:, :, 0, 0:2, :], hw.at[:, :, 0, SUBS - 2 : SUBS, :], -1, 0)
    send(xe.at[:, :, 1, SUBS - 2 : SUBS, :], hw.at[:, :, 1, 0:2, :], 1, 0)
    send(xe.at[:, :, 1, 0:1, :], hw.at[:, :, 1, SUBS - 1 : SUBS, :], -1, 0)
    send(xe.at[:, :, 0, SUBS - 1 : SUBS, :], hw.at[:, :, 0, 0:1, :], 1, 0)

    core = slice(0, rows)
    loads[4].wait()
    for p in range(2):
        for sub in range(2):
            c_own[2 * p + sub, core] = packed([ends(x, v, p, sub) for v in range(vectors)])
    c_own[4, core] = packed([ends(f, k) for k in range(5)])
    send(c_own.at[:, core, :], c_right.at[:, core, :], 0, -1)
    send(c_own.at[:, core, :], c_left.at[:, core, :], 0, 1)

    def fill(g, bent, fields, t):
        for i, item in enumerate(fields):
            g[3, i, :, tile(t)] = item
            g[0, i, :, tile(t)] = item * SIXTH
            g[1, i, :, tile(t)] = item * (2.0 * SIXTH)
            if i < 5:
                g[2, i, :, tile(t)] = item * (bent[i] * SIXTH * SIXTH)

    def turned(items, shift):
        size = items[0].shape
        lane = lax.broadcasted_iota(jnp.int32, size, 1)
        rolled = [pltpu.roll(t, shift % LANES, 1) for t in items]
        if shift > 0:
            return [jnp.where(lane == 0, rolled[(t - 1) % tiles], rolled[t]) for t in range(tiles)]
        return [
            jnp.where(lane == LANES - 1, rolled[(t + 1) % tiles], rolled[t]) for t in range(tiles)
        ]

    sub_r = lax.broadcasted_iota(jnp.int32, (rows, LANES), 0)
    lane_r = lax.broadcasted_iota(jnp.int32, (rows, LANES), 1)
    shifted = turned([f[2, :, tile(t)] for t in range(tiles)], -1)
    for t in range(tiles):
        inner = jnp.where(sub_r == 0, 0.0, f[1, :, tile(t)])
        fill(
            gb,
            BENT_INNER,
            (f[0, :, tile(t)], inner, f[2, :, tile(t)], down(inner), shifted[t],
             f[3, :, tile(t)], f[4, :, tile(t)]),
            t,
        )
        for k in range(4):
            fo[k, :, tile(t)] = window_a(f[k, :, tile(t)])
        fo[4, :, tile(t)] = window_b(f[4, :, tile(t)])

    def inner_terms(a, b, w):
        left, right = turned(b, 1), turned(a, -1)
        found = []
        for t in range(tiles):
            f0, f1, f2, d1, d2 = (gb[w, i, :, tile(t)] for i in range(5))
            found.append((f0 * b[t], f1 * up(b[t]) + f2 * left[t], f0 * a[t], d1 * down(a[t]) + d2 * right[t]))
        return found

    def window_terms(a, b, w, leak=None):
        b_up, a_down = [down(t) for t in b], [up(t) for t in a]
        left, right = turned(b_up, 1), turned(a_down, -1)
        found = []
        for t in range(tiles):
            f0, f1, f2, d0, d2 = (gw[w, i, :, tile(t)] for i in range(5))
            over_a = a[t] if leak is None else a[t] + leak[0][t]
            over_b = b[t] if leak is None else b[t] + leak[1][t]
            found.append((f0 * b_up[t], f1 * over_b + f2 * left[t], d0 * a_down[t], f1 * over_a + d2 * right[t]))
        return found

    def both(items):
        return [item[0] for item in items], [item[1] for item in items]

    def at_tile(pair, t):
        return pair[0][t], pair[1][t]

    def chains(q0, terms, g, leaks):
        def on(w, t):
            return g[w, 5, :, tile(t)], g[w, 6, :, tile(t)]

        def less(pair, other, times=None):
            return both(
                [
                    tuple(
                        one - (two if times is None else two * times)
                        for one, two in zip(at_tile(pair, t), at_tile(other, t))
                    )
                    for t in range(tiles)
                ]
            )

        def stepped(pair, found, w):
            return both([energy(at_tile(pair, t), found[t], on(w, t)) for t in range(tiles)])

        t0 = terms(*q0, 3, *leaks[0:1])
        m0 = both([speed(item) for item in t0])
        q1 = stepped(q0, t0, 3)
        t1 = terms(*q1, 3, *leaks[1:2])
        n1 = both([speed(item) for item in t1])
        q2 = less(stepped(q1, t1, 3), q0, HALF_SQUARE)
        n2 = both([(a0 + a12, -(b0 + b12)) for a0, a12, b0, b12 in terms(*q2, 2)])
        m1 = stepped(m0, terms(*m0, 0, *leaks[2:3]), 0)
        m2 = less(stepped(m1, terms(*m1, 1), 1), m0)
        return q1, (m0, m1, m2, n1, n2)

    def block_edge(t, size):
        lane = lax.broadcasted_iota(jnp.int32, size, 1)
        keep_lanes = None
        if t == 0:
            keep_lanes = lane >= EDGE
        if t == last:
            end = lane < LANES - EDGE
            keep_lanes = end if keep_lanes is None else keep_lanes & end
        return keep_lanes

    def lefts_inside(at, t):
        mask = block_edge(t, (SUBS, LANES))
        return at[:MOMENTS] if mask is None else masked(mask, at)

    def one_vector(v, carry):
        for p in range(2):
            q0 = tuple([x[v, p, sub, :, tile(t)] for t in range(tiles)] for sub in range(2))
            q1, slots = chains(q0, inner_terms, gb, ())
            for s, pair in enumerate(slots):
                for t in range(tiles):
                    for sub in range(2):
                        keep[s, p, sub, :, tile(t)] = pair[sub][t]
                    bw[v, p, s, 0, :, tile(t)] = window_a(pair[0][t])
                    bw[v, p, s, 1, :, tile(t)] = window_b(pair[1][t])
            for s, pair in enumerate((q0, q1, slots[0])):
                for t in range(tiles):
                    lk[v, p, s, 0, :, tile(t)] = jnp.where(sub8 == 1, window_a(pair[0][t]), 0.0)
                    lk[v, p, s, 1, :, tile(t)] = jnp.where(sub8 == 6, window_b(pair[1][t]), 0.0)
            for buf, pair in ((lbuf, slots[2]), (rbuf, slots[4])):
                for sub in range(2):
                    for t in range(tiles):
                        value = -pair[sub][t] if p == 0 else pair[sub][t]
                        buf[v, 1 - p, sub, :, tile(t)] = value.astype(jnp.bfloat16)

        for r in range(0, rows, SUBS):
            band = slice(r, r + SUBS)
            sums = [[[acc[p, n, m, band, :] for m in range(MOMENTS)] for n in range(MOMENTS)] for p in range(2)]
            for sub in range(2):
                for t in range(tiles):
                    at = [[keep[s, p, sub, band, tile(t)] for p in range(2)] for s in range(SLOTS)]
                    add_products(sums, lefts_inside(at, t), rights_of(at))
            for p, n, m in each_sum():
                acc[p, n, m, band, :] = sums[p][n][m]
        return carry

    lax.fori_loop(0, vectors, one_vector, 0)

    for copy in sends[:4]:
        copy.wait_recv()

    taken_a = (sub8 < 1) | (sub8 >= SUBS - 2)
    taken_b = (sub8 < 2) | (sub8 >= SUBS - 1)
    cut = (sub8 == 3) | (sub8 == SUBS - 1)
    windows = [
        [jnp.where(taken_b if k == 4 else taken_a, fw[k, :, tile(t)], fo[k, :, tile(t)]) for t in range(tiles)]
        for k in range(5)
    ]
    for k in (0, 2):
        windows[k] = [jnp.where(cut, 0.0, t) for t in windows[k]]
    far = turned([up(t) for t in windows[2]], -1)
    for t in range(tiles):
        fill(
            gw,
            BENT_WINDOW,
            (windows[0][t], windows[1][t], windows[2][t], up(windows[0][t]), far[t], windows[3][t], windows[4][t]),
            t,
        )

    for copy in sends[4:10] + sends[14:16]:
        copy.wait_recv()

    tlane = lax.broadcasted_iota(jnp.int32, (tall, LANES), 1)
    tspot = lax.rem(tlane, GROUP)
    from_left = (tlane < HALF) & (tspot < GROUP // 2)
    from_right = (tlane >= HALF) & (tspot >= GROUP // 2)

    def joined(k):
        return jnp.where(from_left, c_left[k], jnp.where(from_right, c_right[k], c_own[k]))

    field_tile = joined(4)
    place = (tlane // HALF) * HALF + tspot
    for k in range(5):
        hf[k] = jnp.take_along_axis(field_tile, place + GROUP * k, axis=1)
    hf[5] = down(hf[1])
    hf[6] = jnp.take_along_axis(field_tile, lax.rem(place + (2 * GROUP + 1), LANES), axis=1)
    h_on = (hf[3], hf[4])

    def rim_terms(a, b):
        f0, f1, f2, d1, d2 = hf[0], hf[1], hf[2], hf[5], hf[6]
        return (
            f0 * b, f1 * up(b) + f2 * pltpu.roll(b, 1, 1),
            f0 * a, d1 * down(a) + d2 * pltpu.roll(a, LANES - 1, 1),
        )

    for p in range(2):
        q0 = (joined(2 * p), joined(2 * p + 1))
        t0 = rim_terms(*q0)
        m0 = speed(t0)
        q1 = energy(q0, t0, h_on)
        t1 = rim_terms(*q1)
        n1 = speed(t1)
        h1 = energy(q1, t1, h_on)
        q2 = (h1[0] - HALF_SQUARE * q0[0], h1[1] - HALF_SQUARE * q0[1])
        n2 = tuple(item / HALF_SQUARE for item in speed(rim_terms(*q2)))
        m1 = energy(m0, rim_terms(*m0), h_on, SIXTH)
        h2 = energy(m1, rim_terms(*m1), h_on, 2.0 * SIXTH)
        m2 = (h2[0] - m0[0], h2[1] - m0[1])
        for s, pair in enumerate((m0, m1, m2, n1, n2)):
            for sub in range(2):
                cv[s, p, sub] = pair[sub][0:rows]

    spot8 = lax.rem(lane8, GROUP)
    rim_lanes = ((lane8 < HALF) & ((spot8 == 4) | (spot8 == 5))) | (
        (lane8 >= HALF) & ((spot8 == 2) | (spot8 == 3))
    )

    for copy in sends[10:14]:
        copy.wait_recv()

    def one_window(v):
        for p in range(2):
            q0 = tuple([hw[v, p, sub, :, tile(t)] for t in range(tiles)] for sub in range(2))
            leaks = [
                tuple([lk[v, p, s, sub, :, tile(t)] for t in range(tiles)] for sub in range(2))
                for s in range(3)
            ]
            _, slots = chains(q0, window_terms, gw, leaks)
            for s, pair in enumerate(slots):
                for sub in range(2):
                    for t in range(tiles):
                        bw[v, p, s, sub, :, tile(t)] = bw[v, p, s, sub, :, tile(t)] + pair[sub][t]

    def some_windows(i, carry):
        for j in range(UNROLL):
            one_window(i * UNROLL + j)
        return carry

    if UNROLL == vectors:
        some_windows(0, 0)
    else:
        lax.fori_loop(0, vectors // UNROLL, some_windows, 0)

    def none():
        zero = jnp.zeros((SUBS, LANES), jnp.float32)
        return [[[zero for _ in range(MOMENTS)] for _ in range(MOMENTS)] for _ in range(2)]

    for sub in range(2):
        sums = none()
        for v in range(vectors):
            for t in range(tiles):
                at = [[bw[v, p, s, sub, :, tile(t)] for p in range(2)] for s in range(SLOTS)]
                add_products(sums, lefts_inside(at, t), rights_of(at))
        for p, n, m in each_sum():
            acw[sub, p, n, m] = sums[p][n][m]

    for r in range(0, rows, SUBS):
        band = slice(r, r + SUBS)
        sums = none()
        for sub in range(2):
            at = [[cv[s, p, sub, band] for p in range(2)] for s in range(SLOTS)]
            add_products(sums, masked(rim_lanes, at), rights_of(at))
        for p, n, m in each_sum():
            value = acc[p, n, m, band, :]
            if r == 0 or r == rows - SUBS:
                over = acw[0, p, n, m] + pltpu.roll(acw[1, p, n, m], SUBS - 1, 0)
                if r == 0:
                    value = jnp.where(sub8 < EDGE, pltpu.roll(over, SUBS - 1, 0), value)
                if r == rows - SUBS:
                    value = jnp.where(sub8 >= SUBS - EDGE, pltpu.roll(over, 2, 0), value)
            value = value + sums[p][n][m]
            acc[p, n, m, band, :] = value * SIXTH if m == 1 else value

    count = 2 * MOMENTS * MOMENTS * rows
    rest = acc[...].reshape(count, LANES)
    ones = jnp.ones((SUBS, LANES), jnp.bfloat16)
    total = None
    for _ in range(3):
        piece = rest.astype(jnp.bfloat16)
        rest = rest - piece.astype(jnp.float32)
        part = lax.dot_general(
            ones, piece, (((1,), (1,)), ((), ())), preferred_element_type=jnp.float32
        )
        total = part if total is None else total + part
    part_mom[0] = total
    swaps = []
    for d in range(1, gyn):
        copy = pltpu.make_async_remote_copy(
            src_ref=part_mom.at[0, 0:1], dst_ref=part_mom.at[d, 0:1],
            send_sem=msend_sem.at[d - 1], recv_sem=mrecv_sem.at[d - 1],
            device_id=peer(0, d), device_id_type=MESH,
        )
        copy.start()
        swaps.append(copy)

    def patch(v, carry):
        turn_first = lax.rem(2 * LANES - GROUP // 2 - GROUP * v, LANES)
        turn_last = lax.rem(2 * LANES - GROUP // 2 + HALF - GROUP * v, LANES)
        for p in range(2):
            for sub in range(2):
                for s, buf in ((2, lbuf), (4, rbuf)):
                    side = cv[s, p, sub]
                    for t in range(tiles):
                        value = buf[v, 1 - p, sub, :, tile(t)].astype(jnp.float32)
                        over = bw[v, p, s, sub, :, tile(t)]
                        edge = -side if p == 0 else side
                        over = -over if p == 0 else over
                        top = jnp.where(sub8 < EDGE, pltpu.roll(over, SUBS - 1 - sub, 0), value[0:SUBS])
                        bottom = jnp.where(
                            sub8 >= SUBS - EDGE, pltpu.roll(over, 2 - sub, 0), value[rows - SUBS : rows]
                        )
                        value = jnp.concatenate([top, value[SUBS : rows - SUBS], bottom] if rows > 2 * SUBS else [top, bottom], 0)
                        if t == 0:
                            value = jnp.where(lane_r < EDGE, pltpu.roll(edge, turn_first, 1), value)
                        if t == last:
                            value = jnp.where(lane_r >= LANES - EDGE, pltpu.roll(edge, turn_last, 1), value)
                        buf[v, 1 - p, sub, :, tile(t)] = value.astype(jnp.bfloat16)
        return carry

    lax.fori_loop(0, vectors, patch, 0)

    for copy in swaps:
        copy.wait_recv()
    total = part_mom[0]
    for d in range(1, gyn):
        total = total + part_mom[d]
    out_mom[...] = total / float(vectors * cols * gyn)
    for copy in sends + swaps:
        copy.wait_send()


def writer(total, lbuf, rbuf, out_mom, out_left, out_right, mom, out_sem):
    outs = [
        pltpu.make_async_copy(lbuf, out_left, out_sem.at[0]),
        pltpu.make_async_copy(rbuf, out_right, out_sem.at[1]),
    ]
    for copy in outs:
        copy.start()
    rows = mom.shape[3]
    for p in range(2):
        for n in range(MOMENTS):
            for m in range(MOMENTS):
                k = (p * MOMENTS + n) * MOMENTS + m
                mom[n, m, p : p + 1, :] = total[0:1, k * rows : (k + 1) * rows]
    outs.append(pltpu.make_async_copy(mom, out_mom, out_sem.at[2]))
    outs[2].start()
    for copy in outs:
        copy.wait()


def solution(mesh):
    gxn, gyn = mesh.shape["gx"], mesh.shape["gy"]

    def per_device(vectors, bonds, onsite):
        count, _, _, rows, cols = vectors.shape
        tall = rows + 8
        f32 = jnp.float32
        in_hbm = pl.BlockSpec(memory_space=pltpu.HBM)
        last = jax.ShapeDtypeStruct(vectors.shape, jnp.bfloat16)
        sends = 16
        in_vmem = pl.BlockSpec(memory_space=pltpu.VMEM)
        sums = (8, 2 * MOMENTS * MOMENTS * rows)
        made = pl.pallas_call(
            functools.partial(kernel, gxn, gyn),
            out_shape=(
                pltpu.VMEM(sums, f32),
                pltpu.VMEM(vectors.shape, jnp.bfloat16),
                pltpu.VMEM(vectors.shape, jnp.bfloat16),
            ),
            in_specs=[in_hbm] * 3,
            out_specs=(in_vmem,) * 3,
            scratch_shapes=[
                pltpu.VMEM(vectors.shape, f32),
                pltpu.VMEM((count, 2, 2, SUBS, cols), f32),
                pltpu.VMEM((5, rows, cols), f32),
                pltpu.VMEM((5, SUBS, cols), f32),
                pltpu.VMEM((5, SUBS, cols), f32),
                pltpu.VMEM((count, 2, 2, SUBS, cols), f32),
                pltpu.VMEM((4, 7, rows, cols), f32),
                pltpu.VMEM((4, 7, SUBS, cols), f32),
                pltpu.VMEM((5, SUBS, LANES), f32),
                pltpu.VMEM((5, tall, LANES), f32),
                pltpu.VMEM((5, tall, LANES), f32),
                pltpu.VMEM((5, tall, LANES), f32),
                pltpu.VMEM((7, tall, LANES), f32),
                pltpu.VMEM((SLOTS, 2, 2, rows, LANES), f32),
                pltpu.VMEM((count, 2, SLOTS, 2, SUBS, cols), f32),
                pltpu.VMEM((count, 2, 3, 2, SUBS, cols), f32),
                pltpu.VMEM((SLOTS, 2, 2, rows, cols), f32),
                pltpu.VMEM((2, MOMENTS, MOMENTS, rows, LANES), f32),
                pltpu.VMEM((2, 2, MOMENTS, MOMENTS, SUBS, LANES), f32),
                pltpu.VMEM((gyn, *sums), f32),
                pltpu.SemaphoreType.DMA((5,)),
                pltpu.SemaphoreType.DMA((sends,)),
                pltpu.SemaphoreType.DMA((sends,)),
                pltpu.SemaphoreType.DMA((gyn - 1,)),
                pltpu.SemaphoreType.DMA((gyn - 1,)),
            ],
            compiler_params=pltpu.CompilerParams(
                collective_id=0, has_side_effects=True, vmem_limit_bytes=GRANT
            ),
        )(*(pltpu.with_memory_space_constraint(array, pltpu.HBM) for array in (vectors, bonds, onsite)))
        made = [pltpu.with_memory_space_constraint(array, pltpu.VMEM) for array in made]
        moments, left, right = pl.pallas_call(
            writer,
            out_shape=(
                jax.ShapeDtypeStruct((MOMENTS, MOMENTS, 2, rows), f32), last, last,
            ),
            in_specs=[in_vmem] * 3,
            out_specs=(in_hbm,) * 3,
            scratch_shapes=[
                pltpu.VMEM((MOMENTS, MOMENTS, 2, rows), f32),
                pltpu.SemaphoreType.DMA((3,)),
            ],
            compiler_params=pltpu.CompilerParams(vmem_limit_bytes=GRANT),
        )(*made)
        return jnp.transpose(moments, (2, 0, 1, 3)), left, right

    return jax.shard_map(
        per_device,
        mesh=mesh,
        in_specs=(P(None, None, None, "gx", "gy"), P(None, "gx", "gy"), P(None, "gx", "gy")),
        out_specs=(
            P(None, None, None, "gx"),
            P(None, None, None, "gx", "gy"),
            P(None, None, None, "gx", "gy"),
        ),
        check_vma=False,
    )
```

time: 18.4 us -> 16.3 us (0.89)
  Pallas kernels: 17.6 us -> 15.5 us
    pallas_call x1, Pallas kernels: 16.8 us -> 14.6 us  [per_device(): pl.pallas_call(functools.partial(kernel, gxn, gyn), out_shape=(pltpu.VMEM...]
where the time goes in v2:
time: 16.3 us; the launch traced here: 16.1 us
  Pallas kernels  15.5 us (95%)
  between operations  0.64 us (4%)
    pallas_call x1, Pallas kernels, per_device(): pl.pallas_call(functools.partial(kernel, gxn, gyn), out_shape=(pltpu.VMEM...  14.6 us
    pallas_call x1, Pallas kernels, per_device(): pl.pallas_call(writer, out_shape=(jax.ShapeDtypeStruct((MOMENTS, MOMENTS,...  0.82 us

profile of v2, /device:TPU:0, one launch (start us, length us, event | category | flops | bytes accessed | tf_op | source)
XLA Modules:
  0.0 16.1 jit_solution(1579261021406092424)
XLA Ops:
  0.6 14.6 %shard_map.58 = (f32[8,288]{1,0:T(8,128)S(1)}, bf16[8,2,2,16,256]{4,3,2,1,0:T(8,128)(2,1)S(1)}, bf16[8,2,2,16,256]{4,3,2,1,0:T(8,128)(2,1)S(1)}) custom-call(f32[8,2,2,16,256]{4,3,2,1,0:T(8,128)} %vec.1, f32[3,16,256]{2,1,0:T(8,128)} %bonds.1, f32[2,16,256]{2,1,0:T(8,128)} %onsite.1), custom_call_target="tpu_custom_call" | custom-call | tf_op jit(solution)/shard_map/pallas_call | solution.py:530
  15.3 0.8 %shard_map.59 = (f32[3,3,2,16]{3,2,1,0:T(2,128)}, bf16[8,2,2,16,256]{4,3,2,1,0:T(8,128)(2,1)}, bf16[8,2,2,16,256]{4,3,2,1,0:T(8,128)(2,1)}) custom-call(f32[8,288]{1,0:T(8,128)S(1)} %get-tuple-element.9.total, bf16[8,2,2,16,256]{4,3,2,1,0:T(8,128)(2,1)S(1)} %get-tuple-element.10.lbuf, bf16[8,2,2,16,256]{4,3,2,1,0:T(8,128)(2,1)S(1)} %get-tuple-element.11.rbuf), custom_call_target="tpu_custom_call" | custom-call | tf_op jit(solution)/shard_map/pallas_call | solution.py:571

commit v3 on v2

--- a/solution.py
+++ b/solution.py
@@ -14,7 +14,6 @@
 LANES = 128
 SUBS = 8
 SLOTS = 5
-UNROLL = 8
 GRANT = 32 * 1024 * 1024
 MESH = pl.DeviceIdType.MESH
 SIXTH = 1.0 / SCALE
@@ -68,7 +67,7 @@
 
 def kernel(
     gxn, gyn, vec, bonds, onsite, out_mom, lbuf, rbuf,
-    x, xe, f, fw, fo, hw, gb, gw, cc, c_own, c_left, c_right, hf, cv, bw, lk, keep, acc, acw, part_mom,
+    x, xe, f, fw, fo, hw, gb, gw, cc, c_own, c_left, c_right, hf, cv, bw, lk, state, keep, acc, part_mom,
     load_sem, send_sem, recv_sem, msend_sem, mrecv_sem,
 ):
     vectors, _, _, rows, cols = vec.shape
@@ -80,6 +79,13 @@
 
     def peer(dx, dy):
         return (lax.rem(gx + dx + gxn, gxn), lax.rem(gy + dy + gyn, gyn))
+
+    barrier = pltpu.get_barrier_semaphore()
+    near = [(dx % gxn, dy % gyn) for dx in (-1, 1) for dy in (0, 1, -1)]
+    near += [(0, dy) for dy in range(gyn)]
+    near = [one for k, one in enumerate(near) if one != (0, 0) and one not in near[:k]]
+    for dx, dy in near:
+        pl.semaphore_signal(barrier, inc=1, device_id=peer(dx, dy), device_id_type=MESH)
 
     low, high = slice(0, EDGE), slice(SUBS - EDGE, SUBS)
     loads = [
@@ -94,13 +100,6 @@
     for copy in loads:
         copy.start()
 
-    barrier = pltpu.get_barrier_semaphore()
-    near = [(0, dy) for dy in range(gyn)]
-    near += [(dx % gxn, dy % gyn) for dx in (-1, 1) for dy in (-1, 0, 1)]
-    near = [one for k, one in enumerate(near) if one != (0, 0) and one not in near[:k]]
-    for dx, dy in near:
-        pl.semaphore_signal(barrier, inc=1, device_id=peer(dx, dy), device_id_type=MESH)
-
     hw[:, :, 0, 1 : SUBS - EDGE, :] = jnp.zeros((vectors, 2, SUBS - EDGE - 1, cols), jnp.float32)
     hw[:, :, 1, EDGE : SUBS - 1, :] = jnp.zeros((vectors, 2, SUBS - EDGE - 1, cols), jnp.float32)
     acc[...] = jnp.zeros_like(acc)
@@ -112,8 +111,8 @@
             src_ref=src, dst_ref=dst, send_sem=send_sem.at[n], recv_sem=recv_sem.at[n],
             device_id=peer(dx, dy), device_id_type=MESH,
         )
-        copy.start()
         sends.append(copy)
+        return copy
 
     def packed(items):
         count = items[0][0].shape[0]
@@ -122,9 +121,10 @@
         total = None
         for k, (first, final) in enumerate(items):
             both = jnp.where(lane < HALF, first, final)
-            moved = pltpu.roll(both, GROUP * k + GROUP // 2, 1)
+            place = lax.rem(spot + (2 * LANES - GROUP * k - GROUP // 2), LANES)
+            moved = jnp.take_along_axis(both, place, axis=1)
             total = jnp.where(spot // GROUP == k, moved, total) if k else moved
-        return jnp.where(lane < HALF, total, pltpu.roll(total, HALF, 1))
+        return total
 
     def ends(ref, *index):
         return ref[(*index, slice(None), slice(0, LANES))], ref[
@@ -154,29 +154,15 @@
         return jnp.where(sub8 < 4, t[0:SUBS], t[rows - SUBS : rows])
 
     cc[4] = packed([tuple(rim_rows(t) for t in ends(f, k)) for k in range(5)])
-    pl.semaphore_wait(barrier, len(near))
-
-    send(f.at[0:4, 0:2, :], fw.at[0:4, SUBS - 2 : SUBS, :], -1, 0)
-    send(f.at[4:5, 0:1, :], fw.at[4:5, SUBS - 1 : SUBS, :], -1, 0)
-    send(f.at[0:4, rows - 1 : rows, :], fw.at[0:4, 0:1, :], 1, 0)
-    send(f.at[4:5, rows - 2 : rows, :], fw.at[4:5, 0:2, :], 1, 0)
-    past, ahead = slice(rows, rows + EDGE), slice(tall - EDGE, tall)
-    for dst, dy in ((c_right, -1), (c_left, 1), (c_own, 0)):
-        send(cc.at[:, low, :], dst.at[:, past, :], -1, dy)
-        send(cc.at[:, high, :], dst.at[:, ahead, :], 1, dy)
-    send(xe.at[:, :, 0, 0:2, :], hw.at[:, :, 0, SUBS - 2 : SUBS, :], -1, 0)
-    send(xe.at[:, :, 1, SUBS - 2 : SUBS, :], hw.at[:, :, 1, 0:2, :], 1, 0)
-    send(xe.at[:, :, 1, 0:1, :], hw.at[:, :, 1, SUBS - 1 : SUBS, :], -1, 0)
-    send(xe.at[:, :, 0, SUBS - 1 : SUBS, :], hw.at[:, :, 0, 0:1, :], 1, 0)
-
+    lane_r = lax.broadcasted_iota(jnp.int32, (rows, LANES), 1)
     core = slice(0, rows)
-    loads[4].wait()
-    for p in range(2):
-        for sub in range(2):
-            c_own[2 * p + sub, core] = packed([ends(x, v, p, sub) for v in range(vectors)])
-    c_own[4, core] = packed([ends(f, k) for k in range(5)])
-    send(c_own.at[:, core, :], c_right.at[:, core, :], 0, -1)
-    send(c_own.at[:, core, :], c_left.at[:, core, :], 0, 1)
+
+    def pack_block():
+        loads[4].wait()
+        for p in range(2):
+            for sub in range(2):
+                c_own[2 * p + sub, core] = packed([ends(x, v, p, sub) for v in range(vectors)])
+        c_own[4, core] = packed([ends(f, k) for k in range(5)])
 
     def fill(g, bent, fields, t):
         for i, item in enumerate(fields):
@@ -191,26 +177,10 @@
         lane = lax.broadcasted_iota(jnp.int32, size, 1)
         rolled = [pltpu.roll(t, shift % LANES, 1) for t in items]
         if shift > 0:
-            return [jnp.where(lane == 0, rolled[(t - 1) % tiles], rolled[t]) for t in range(tiles)]
+            return rolled[:1] + [jnp.where(lane == 0, rolled[t - 1], rolled[t]) for t in range(1, tiles)]
         return [
-            jnp.where(lane == LANES - 1, rolled[(t + 1) % tiles], rolled[t]) for t in range(tiles)
-        ]
-
-    sub_r = lax.broadcasted_iota(jnp.int32, (rows, LANES), 0)
-    lane_r = lax.broadcasted_iota(jnp.int32, (rows, LANES), 1)
-    shifted = turned([f[2, :, tile(t)] for t in range(tiles)], -1)
-    for t in range(tiles):
-        inner = jnp.where(sub_r == 0, 0.0, f[1, :, tile(t)])
-        fill(
-            gb,
-            BENT_INNER,
-            (f[0, :, tile(t)], inner, f[2, :, tile(t)], down(inner), shifted[t],
-             f[3, :, tile(t)], f[4, :, tile(t)]),
-            t,
-        )
-        for k in range(4):
-            fo[k, :, tile(t)] = window_a(f[k, :, tile(t)])
-        fo[4, :, tile(t)] = window_b(f[4, :, tile(t)])
+            jnp.where(lane == LANES - 1, rolled[t + 1], rolled[t]) for t in range(last)
+        ] + rolled[last:]
 
     def inner_terms(a, b, w):
         left, right = turned(b, 1), turned(a, -1)
@@ -266,19 +236,25 @@
         m2 = less(stepped(m1, terms(*m1, 1), 1), m0)
         return q1, (m0, m1, m2, n1, n2)
 
-    def block_edge(t, size):
-        lane = lax.broadcasted_iota(jnp.int32, size, 1)
+    def inside_lanes(t):
         keep_lanes = None
         if t == 0:
-            keep_lanes = lane >= EDGE
+            keep_lanes = lane8 >= EDGE
         if t == last:
-            end = lane < LANES - EDGE
+            end = lane8 < LANES - EDGE
             keep_lanes = end if keep_lanes is None else keep_lanes & end
         return keep_lanes
 
-    def lefts_inside(at, t):
-        mask = block_edge(t, (SUBS, LANES))
-        return at[:MOMENTS] if mask is None else masked(mask, at)
+    def inside(sub, r, t):
+        keep_cells = inside_lanes(t)
+        cuts = []
+        if r == 0:
+            cuts.append(sub8 >= EDGE - sub)
+        if r == rows - SUBS:
+            cuts.append(sub8 < SUBS - 1 - sub)
+        for one in cuts:
+            keep_cells = one if keep_cells is None else keep_cells & one
+        return keep_cells
 
     def one_vector(v, carry):
         for p in range(2):
@@ -288,8 +264,13 @@
                 for t in range(tiles):
                     for sub in range(2):
                         keep[s, p, sub, :, tile(t)] = pair[sub][t]
-                    bw[v, p, s, 0, :, tile(t)] = window_a(pair[0][t])
-                    bw[v, p, s, 1, :, tile(t)] = window_b(pair[1][t])
+                    a, b = pair[0][t], pair[1][t]
+                    ends_a, ends_b = (a[0:SUBS], a[rows - SUBS : rows]), (b[0:SUBS], b[rows - SUBS : rows])
+                    over = jnp.where(sub8 == 3, pltpu.roll(ends_b[0], 3, 0), ends_b[1])
+                    over = jnp.where(sub8 == 5, pltpu.roll(ends_a[1], SUBS - 2, 0), over)
+                    bw[v, p, s, :, tile(t)] = jnp.where(
+                        (sub8 == 1) | (sub8 == 2), pltpu.roll(ends_a[0], 1, 0), over
+                    )
             for s, pair in enumerate((q0, q1, slots[0])):
                 for t in range(tiles):
                     lk[v, p, s, 0, :, tile(t)] = jnp.where(sub8 == 1, window_a(pair[0][t]), 0.0)
@@ -306,14 +287,78 @@
             for sub in range(2):
                 for t in range(tiles):
                     at = [[keep[s, p, sub, band, tile(t)] for p in range(2)] for s in range(SLOTS)]
-                    add_products(sums, lefts_inside(at, t), rights_of(at))
+                    mask = inside(sub, r, t)
+                    add_products(sums, at[:MOMENTS] if mask is None else masked(mask, at), rights_of(at))
             for p, n, m in each_sum():
                 acc[p, n, m, band, :] = sums[p][n][m]
         return carry
 
-    lax.fori_loop(0, vectors, one_vector, 0)
-
-    for copy in sends[:4]:
+    def own_block():
+        sub_r = lax.broadcasted_iota(jnp.int32, (rows, LANES), 0)
+        shifted = turned([f[2, :, tile(t)] for t in range(tiles)], -1)
+        for t in range(tiles):
+            inner = jnp.where(sub_r == 0, 0.0, f[1, :, tile(t)])
+            fill(
+                gb,
+                BENT_INNER,
+                (f[0, :, tile(t)], inner, f[2, :, tile(t)], down(inner), shifted[t],
+                 f[3, :, tile(t)], f[4, :, tile(t)]),
+                t,
+            )
+            for k in range(4):
+                fo[k, :, tile(t)] = window_a(f[k, :, tile(t)])
+            fo[4, :, tile(t)] = window_b(f[4, :, tile(t)])
+        lax.fori_loop(0, vectors, one_vector, 0)
+
+    early = gx == 0
+
+    @pl.when(early)
+    def _():
+        pack_block()
+        own_block()
+
+    pl.semaphore_wait(barrier, len(near))
+
+    past, ahead = slice(rows, rows + EDGE), slice(tall - EDGE, tall)
+    sides = [
+        send(c_own.at[:, core, :], c_right.at[:, core, :], 0, -1),
+        send(c_own.at[:, core, :], c_left.at[:, core, :], 0, 1),
+    ]
+    rims = [
+        send(f.at[0:4, rows - 1 : rows, :], fw.at[0:4, 0:1, :], 1, 0),
+        send(f.at[4:5, rows - 2 : rows, :], fw.at[4:5, 0:2, :], 1, 0),
+    ]
+    for dst, dy in ((c_right, -1), (c_left, 1), (c_own, 0)):
+        rims.append(send(cc.at[:, high, :], dst.at[:, ahead, :], 1, dy))
+    rims += [
+        send(xe.at[:, :, 1, SUBS - 2 : SUBS, :], hw.at[:, :, 1, 0:2, :], 1, 0),
+        send(xe.at[:, :, 0, SUBS - 1 : SUBS, :], hw.at[:, :, 0, 0:1, :], 1, 0),
+        send(f.at[0:4, 0:2, :], fw.at[0:4, SUBS - 2 : SUBS, :], -1, 0),
+        send(f.at[4:5, 0:1, :], fw.at[4:5, SUBS - 1 : SUBS, :], -1, 0),
+    ]
+    for dst, dy in ((c_right, -1), (c_left, 1), (c_own, 0)):
+        rims.append(send(cc.at[:, low, :], dst.at[:, past, :], -1, dy))
+    rims += [
+        send(xe.at[:, :, 0, 0:2, :], hw.at[:, :, 0, SUBS - 2 : SUBS, :], -1, 0),
+        send(xe.at[:, :, 1, 0:1, :], hw.at[:, :, 1, SUBS - 1 : SUBS, :], -1, 0),
+    ]
+
+    @pl.when(early)
+    def _():
+        for copy in sides:
+            copy.start()
+
+    for copy in rims:
+        copy.start()
+
+    @pl.when(jnp.logical_not(early))
+    def _():
+        pack_block()
+        for copy in sides:
+            copy.start()
+        own_block()
+
+    for copy in sends:
         copy.wait_recv()
 
     taken_a = (sub8 < 1) | (sub8 >= SUBS - 2)
@@ -334,8 +379,6 @@
             t,
         )
 
-    for copy in sends[4:10] + sends[14:16]:
-        copy.wait_recv()
 
     tlane = lax.broadcasted_iota(jnp.int32, (tall, LANES), 1)
     tspot = lax.rem(tlane, GROUP)
@@ -382,45 +425,75 @@
         (lane8 >= HALF) & ((spot8 == 2) | (spot8 == 3))
     )
 
-    for copy in sends[10:14]:
-        copy.wait_recv()
-
-    def one_window(v):
-        for p in range(2):
-            q0 = tuple([hw[v, p, sub, :, tile(t)] for t in range(tiles)] for sub in range(2))
-            leaks = [
-                tuple([lk[v, p, s, sub, :, tile(t)] for t in range(tiles)] for sub in range(2))
-                for s in range(3)
-            ]
-            _, slots = chains(q0, window_terms, gw, leaks)
-            for s, pair in enumerate(slots):
-                for sub in range(2):
-                    for t in range(tiles):
-                        bw[v, p, s, sub, :, tile(t)] = bw[v, p, s, sub, :, tile(t)] + pair[sub][t]
-
-    def some_windows(i, carry):
-        for j in range(UNROLL):
-            one_window(i * UNROLL + j)
-        return carry
-
-    if UNROLL == vectors:
-        some_windows(0, 0)
-    else:
-        lax.fori_loop(0, vectors // UNROLL, some_windows, 0)
 
     def none():
         zero = jnp.zeros((SUBS, LANES), jnp.float32)
         return [[[zero for _ in range(MOMENTS)] for _ in range(MOMENTS)] for _ in range(2)]
 
-    for sub in range(2):
+    from_a = (sub8 == 1) | (sub8 == 2) | (sub8 == 5)
+    planes = [(v, p) for v in range(vectors) for p in range(2)]
+
+    def pair_of(ref, *index):
+        return tuple([ref[(*index, sub, slice(None), tile(t))] for t in range(tiles)] for sub in range(2))
+
+    def on_window(pair, found, w):
+        return both(
+            [
+                energy(at_tile(pair, t), found[t], (gw[w, 5, :, tile(t)], gw[w, 6, :, tile(t)]))
+                for t in range(tiles)
+            ]
+        )
+
+    def put(k, v, p, pair):
+        for sub in range(2):
+            for t in range(tiles):
+                state[k, v, p, sub, :, tile(t)] = pair[sub][t]
+
+    def add(v, p, s, pair):
+        for t in range(tiles):
+            change = jnp.where(from_a, pair[0][t], up(pair[1][t]))
+            bw[v, p, s, :, tile(t)] = bw[v, p, s, :, tile(t)] + change
+
+    def minus(pair, other, times=None):
+        return tuple(
+            [one - (two if times is None else two * times) for one, two in zip(pair[sub], other[sub])]
+            for sub in range(2)
+        )
+
+    for v, p in planes:
+        pair = pair_of(hw, v, p)
+        found = window_terms(*pair, 3, pair_of(lk, v, p, 0))
+        m0 = both([speed(item) for item in found])
+        put(0, v, p, on_window(pair, found, 3))
+        put(1, v, p, m0)
+        add(v, p, 0, m0)
+    for v, p in planes:
+        pair = pair_of(state, 0, v, p)
+        found = window_terms(*pair, 3, pair_of(lk, v, p, 1))
+        add(v, p, 3, both([speed(item) for item in found]))
+        put(2, v, p, minus(on_window(pair, found, 3), pair_of(hw, v, p), HALF_SQUARE))
+    for v, p in planes:
+        pair = pair_of(state, 1, v, p)
+        m1 = on_window(pair, window_terms(*pair, 0, pair_of(lk, v, p, 2)), 0)
+        put(3, v, p, m1)
+        add(v, p, 1, m1)
+    for v, p in planes:
+        found = window_terms(*pair_of(state, 2, v, p), 2)
+        add(v, p, 4, both([(a0 + a12, -(b0 + b12)) for a0, a12, b0, b12 in found]))
+    for v, p in planes:
+        pair = pair_of(state, 3, v, p)
+        add(v, p, 2, minus(on_window(pair, window_terms(*pair, 1), 1), pair_of(state, 1, v, p)))
+
+    found = none()
+    for t in range(tiles):
         sums = none()
         for v in range(vectors):
-            for t in range(tiles):
-                at = [[bw[v, p, s, sub, :, tile(t)] for p in range(2)] for s in range(SLOTS)]
-                add_products(sums, lefts_inside(at, t), rights_of(at))
+            at = [[bw[v, p, s, :, tile(t)] for p in range(2)] for s in range(SLOTS)]
+            add_products(sums, at[:MOMENTS], rights_of(at))
+        mask = inside_lanes(t)
         for p, n, m in each_sum():
-            acw[sub, p, n, m] = sums[p][n][m]
-
+            value = sums[p][n][m] if mask is None else jnp.where(mask, sums[p][n][m], 0.0)
+            found[p][n][m] = value if t == 0 else found[p][n][m] + value
     for r in range(0, rows, SUBS):
         band = slice(r, r + SUBS)
         sums = none()
@@ -428,14 +501,7 @@
             at = [[cv[s, p, sub, band] for p in range(2)] for s in range(SLOTS)]
             add_products(sums, masked(rim_lanes, at), rights_of(at))
         for p, n, m in each_sum():
-            value = acc[p, n, m, band, :]
-            if r == 0 or r == rows - SUBS:
-                over = acw[0, p, n, m] + pltpu.roll(acw[1, p, n, m], SUBS - 1, 0)
-                if r == 0:
-                    value = jnp.where(sub8 < EDGE, pltpu.roll(over, SUBS - 1, 0), value)
-                if r == rows - SUBS:
-                    value = jnp.where(sub8 >= SUBS - EDGE, pltpu.roll(over, 2, 0), value)
-            value = value + sums[p][n][m]
+            value = acc[p, n, m, band, :] + sums[p][n][m]
             acc[p, n, m, band, :] = value * SIXTH if m == 1 else value
 
     count = 2 * MOMENTS * MOMENTS * rows
@@ -449,7 +515,21 @@
             ones, piece, (((1,), (1,)), ((), ())), preferred_element_type=jnp.float32
         )
         total = part if total is None else total + part
-    part_mom[0] = total
+
+    row8 = jnp.where(sub8 < 4, jnp.where(sub8 == 2, 1, 0), jnp.where(sub8 == 6, rows - 2, rows - 1))
+    row8 = jnp.where((sub8 == 0) | (sub8 == 4), -LANES, row8)
+    per = LANES // rows
+    for j in range(0, 2 * MOMENTS * MOMENTS, per):
+        chosen = each_sum()[j : j + per]
+        piece = jnp.zeros((SUBS, LANES), jnp.float32)
+        for k, (p, n, m) in enumerate(chosen):
+            value = jnp.sum(found[p][n][m], axis=1, keepdims=True)
+            piece = jnp.where(lane8 == row8 + k * rows, value * SIXTH if m == 1 else value, piece)
+        for step in (4, 2, 1):
+            piece = piece + pltpu.roll(piece, step, 0)
+        span = slice(j * rows, (j + len(chosen)) * rows)
+        part_mom[0, :, span] = total[:, span] + piece[:, 0 : len(chosen) * rows]
+
     swaps = []
     for d in range(1, gyn):
         copy = pltpu.make_async_remote_copy(
@@ -469,12 +549,14 @@
                     side = cv[s, p, sub]
                     for t in range(tiles):
                         value = buf[v, 1 - p, sub, :, tile(t)].astype(jnp.float32)
-                        over = bw[v, p, s, sub, :, tile(t)]
+                        over = bw[v, p, s, :, tile(t)]
                         edge = -side if p == 0 else side
                         over = -over if p == 0 else over
-                        top = jnp.where(sub8 < EDGE, pltpu.roll(over, SUBS - 1 - sub, 0), value[0:SUBS])
+                        top = jnp.where(
+                            sub8 < EDGE - sub, pltpu.roll(over, SUBS - 1 - 2 * sub, 0), value[0:SUBS]
+                        )
                         bottom = jnp.where(
-                            sub8 >= SUBS - EDGE, pltpu.roll(over, 2 - sub, 0), value[rows - SUBS : rows]
+                            sub8 >= SUBS - 1 - sub, over if sub else pltpu.roll(over, 2, 0), value[rows - SUBS : rows]
                         )
                         value = jnp.concatenate([top, value[SUBS : rows - SUBS], bottom] if rows > 2 * SUBS else [top, bottom], 0)
                         if t == 0:
@@ -551,11 +633,11 @@
                 pltpu.VMEM((5, tall, LANES), f32),
                 pltpu.VMEM((7, tall, LANES), f32),
                 pltpu.VMEM((SLOTS, 2, 2, rows, LANES), f32),
-                pltpu.VMEM((count, 2, SLOTS, 2, SUBS, cols), f32),
+                pltpu.VMEM((count, 2, SLOTS, SUBS, cols), f32),
                 pltpu.VMEM((count, 2, 3, 2, SUBS, cols), f32),
+                pltpu.VMEM((4, count, 2, 2, SUBS, cols), f32),
                 pltpu.VMEM((SLOTS, 2, 2, rows, cols), f32),
                 pltpu.VMEM((2, MOMENTS, MOMENTS, rows, LANES), f32),
-                pltpu.VMEM((2, 2, MOMENTS, MOMENTS, SUBS, LANES), f32),
                 pltpu.VMEM((gyn, *sums), f32),
                 pltpu.SemaphoreType.DMA((5,)),
                 pltpu.SemaphoreType.DMA((sends,)),

time: 16.3 us -> 15.7 us (0.963)
  Pallas kernels: 15.5 us -> 14.9 us
    pallas_call x1, Pallas kernels: 14.6 us -> 14.1 us  [per_device(): pl.pallas_call(functools.partial(kernel, gxn, gyn), out_shape=(pltpu.VMEM...]
where the time goes in v3:
time: 15.7 us; the launch traced here: 15.6 us
  Pallas kernels  14.9 us (95%)
  between operations  0.64 us (4%)
    pallas_call x1, Pallas kernels, per_device(): pl.pallas_call(functools.partial(kernel, gxn, gyn), out_shape=(pltpu.VMEM...  14.1 us
    pallas_call x1, Pallas kernels, per_device(): pl.pallas_call(writer, out_shape=(jax.ShapeDtypeStruct((MOMENTS, MOMENTS,...  0.82 us

profile of v3, /device:TPU:0, one launch (start us, length us, event | category | flops | bytes accessed | tf_op | source)
XLA Modules:
  0.0 15.6 jit_solution(17378262384527663783)
XLA Ops:
  0.6 14.1 %shard_map.58 = (f32[8,288]{1,0:T(8,128)S(1)}, bf16[8,2,2,16,256]{4,3,2,1,0:T(8,128)(2,1)S(1)}, bf16[8,2,2,16,256]{4,3,2,1,0:T(8,128)(2,1)S(1)}) custom-call(f32[8,2,2,16,256]{4,3,2,1,0:T(8,128)} %vec.1, f32[3,16,256]{2,1,0:T(8,128)} %bonds.1, f32[2,16,256]{2,1,0:T(8,128)} %onsite.1), custom_call_target="tpu_custom_call" | custom-call | tf_op jit(solution)/shard_map/pallas_call | solution.py:612
  14.8 0.8 %shard_map.59 = (f32[3,3,2,16]{3,2,1,0:T(2,128)}, bf16[8,2,2,16,256]{4,3,2,1,0:T(8,128)(2,1)}, bf16[8,2,2,16,256]{4,3,2,1,0:T(8,128)(2,1)}) custom-call(f32[8,288]{1,0:T(8,128)S(1)} %get-tuple-element.9.total, bf16[8,2,2,16,256]{4,3,2,1,0:T(8,128)(2,1)S(1)} %get-tuple-element.10.lbuf, bf16[8,2,2,16,256]{4,3,2,1,0:T(8,128)(2,1)S(1)} %get-tuple-element.11.rbuf), custom_call_target="tpu_custom_call" | custom-call | tf_op jit(solution)/shard_map/pallas_call | solution.py:653

commit v4 on v3

--- a/solution.py
+++ b/solution.py
@@ -67,7 +67,7 @@
 
 def kernel(
     gxn, gyn, vec, bonds, onsite, out_mom, lbuf, rbuf,
-    x, xe, f, fw, fo, hw, gb, gw, cc, c_own, c_left, c_right, hf, cv, bw, lk, state, keep, acc, part_mom,
+    x, xe, f, fw, fo, hw, gb, gw, cc, cs, ms, c_own, c_left, c_right, hf, cv, bw, lk, state, keep, acc, part_mom,
     load_sem, send_sem, recv_sem, msend_sem, mrecv_sem,
 ):
     vectors, _, _, rows, cols = vec.shape
@@ -126,6 +126,16 @@
             total = jnp.where(spot // GROUP == k, moved, total) if k else moved
         return total
 
+    def sides_of(four):
+        lane = lax.broadcasted_iota(jnp.int32, four[0].shape, 1)
+        start = lane + jnp.where(lane < HALF, 2, 4)
+        spot = lax.rem(lane, GROUP)
+        total = None
+        for k, one in enumerate(four):
+            moved = jnp.take_along_axis(one, lax.rem(start + (LANES - 2 * k), LANES), axis=1)
+            total = jnp.where(spot // 2 == k, moved, total) if k else moved
+        return total
+
     def ends(ref, *index):
         return ref[(*index, slice(None), slice(0, LANES))], ref[
             (*index, slice(None), slice(cols - LANES, cols))
@@ -149,11 +159,13 @@
     for p in range(2):
         for sub in range(2):
             cc[2 * p + sub] = packed([ends(xe, v, p, sub) for v in range(vectors)])
+    cs[0] = sides_of([cc[k] for k in range(4)])
 
     def rim_rows(t):
         return jnp.where(sub8 < 4, t[0:SUBS], t[rows - SUBS : rows])
 
     cc[4] = packed([tuple(rim_rows(t) for t in ends(f, k)) for k in range(5)])
+    cs[1] = cc[4]
     lane_r = lax.broadcasted_iota(jnp.int32, (rows, LANES), 1)
     core = slice(0, rows)
 
@@ -163,6 +175,8 @@
             for sub in range(2):
                 c_own[2 * p + sub, core] = packed([ends(x, v, p, sub) for v in range(vectors)])
         c_own[4, core] = packed([ends(f, k) for k in range(5)])
+        ms[0] = sides_of([c_own[k, core] for k in range(4)])
+        ms[1] = c_own[4, core]
 
     def fill(g, bent, fields, t):
         for i, item in enumerate(fields):
@@ -321,23 +335,23 @@
 
     past, ahead = slice(rows, rows + EDGE), slice(tall - EDGE, tall)
     sides = [
-        send(c_own.at[:, core, :], c_right.at[:, core, :], 0, -1),
-        send(c_own.at[:, core, :], c_left.at[:, core, :], 0, 1),
+        send(ms, c_right.at[:, core, :], 0, -1),
+        send(ms, c_left.at[:, core, :], 0, 1),
     ]
     rims = [
         send(f.at[0:4, rows - 1 : rows, :], fw.at[0:4, 0:1, :], 1, 0),
         send(f.at[4:5, rows - 2 : rows, :], fw.at[4:5, 0:2, :], 1, 0),
     ]
-    for dst, dy in ((c_right, -1), (c_left, 1), (c_own, 0)):
-        rims.append(send(cc.at[:, high, :], dst.at[:, ahead, :], 1, dy))
+    for src, dst, dy in ((cs, c_right, -1), (cs, c_left, 1), (cc, c_own, 0)):
+        rims.append(send(src.at[:, high, :], dst.at[:, ahead, :], 1, dy))
     rims += [
         send(xe.at[:, :, 1, SUBS - 2 : SUBS, :], hw.at[:, :, 1, 0:2, :], 1, 0),
         send(xe.at[:, :, 0, SUBS - 1 : SUBS, :], hw.at[:, :, 0, 0:1, :], 1, 0),
         send(f.at[0:4, 0:2, :], fw.at[0:4, SUBS - 2 : SUBS, :], -1, 0),
         send(f.at[4:5, 0:1, :], fw.at[4:5, SUBS - 1 : SUBS, :], -1, 0),
     ]
-    for dst, dy in ((c_right, -1), (c_left, 1), (c_own, 0)):
-        rims.append(send(cc.at[:, low, :], dst.at[:, past, :], -1, dy))
+    for src, dst, dy in ((cs, c_right, -1), (cs, c_left, 1), (cc, c_own, 0)):
+        rims.append(send(src.at[:, low, :], dst.at[:, past, :], -1, dy))
     rims += [
         send(xe.at[:, :, 0, 0:2, :], hw.at[:, :, 0, SUBS - 2 : SUBS, :], -1, 0),
         send(xe.at[:, :, 1, 0:1, :], hw.at[:, :, 1, SUBS - 1 : SUBS, :], -1, 0),
@@ -358,7 +372,8 @@
             copy.start()
         own_block()
 
-    for copy in sends:
+    row_sends = rims[5:7] + rims[12:14]
+    for copy in sides + rims[0:5] + rims[7:12]:
         copy.wait_recv()
 
     taken_a = (sub8 < 1) | (sub8 >= SUBS - 2)
@@ -382,13 +397,16 @@
 
     tlane = lax.broadcasted_iota(jnp.int32, (tall, LANES), 1)
     tspot = lax.rem(tlane, GROUP)
-    from_left = (tlane < HALF) & (tspot < GROUP // 2)
-    from_right = (tlane >= HALF) & (tspot >= GROUP // 2)
+    on_left = tlane < HALF
+    from_side = jnp.where(on_left, tspot, tspot - 2) // 2 == 1
+    side = jnp.where(on_left, c_left[0], c_right[0])
+    side_start = tlane + jnp.where(on_left, LANES - 2, LANES - 4)
 
     def joined(k):
-        return jnp.where(from_left, c_left[k], jnp.where(from_right, c_right[k], c_own[k]))
-
-    field_tile = joined(4)
+        moved = jnp.take_along_axis(side, lax.rem(side_start + 2 * k, LANES), axis=1)
+        return jnp.where(from_side, moved, c_own[k])
+
+    field_tile = jnp.where(from_side, jnp.where(on_left, c_left[1], c_right[1]), c_own[4])
     place = (tlane // HALF) * HALF + tspot
     for k in range(5):
         hf[k] = jnp.take_along_axis(field_tile, place + GROUP * k, axis=1)
@@ -429,6 +447,31 @@
     def none():
         zero = jnp.zeros((SUBS, LANES), jnp.float32)
         return [[[zero for _ in range(MOMENTS)] for _ in range(MOMENTS)] for _ in range(2)]
+
+    for r in range(0, rows, SUBS):
+        band = slice(r, r + SUBS)
+        sums = none()
+        for sub in range(2):
+            at = [[cv[s, p, sub, band] for p in range(2)] for s in range(SLOTS)]
+            add_products(sums, masked(rim_lanes, at), rights_of(at))
+        for p, n, m in each_sum():
+            value = acc[p, n, m, band, :] + sums[p][n][m]
+            acc[p, n, m, band, :] = value * SIXTH if m == 1 else value
+
+    count = 2 * MOMENTS * MOMENTS * rows
+    rest = acc[...].reshape(count, LANES)
+    ones = jnp.ones((SUBS, LANES), jnp.bfloat16)
+    total = None
+    for _ in range(3):
+        piece = rest.astype(jnp.bfloat16)
+        rest = rest - piece.astype(jnp.float32)
+        part = lax.dot_general(
+            ones, piece, (((1,), (1,)), ((), ())), preferred_element_type=jnp.float32
+        )
+        total = part if total is None else total + part
+
+    for copy in row_sends:
+        copy.wait_recv()
 
     from_a = (sub8 == 1) | (sub8 == 2) | (sub8 == 5)
     planes = [(v, p) for v in range(vectors) for p in range(2)]
@@ -494,28 +537,6 @@
         for p, n, m in each_sum():
             value = sums[p][n][m] if mask is None else jnp.where(mask, sums[p][n][m], 0.0)
             found[p][n][m] = value if t == 0 else found[p][n][m] + value
-    for r in range(0, rows, SUBS):
-        band = slice(r, r + SUBS)
-        sums = none()
-        for sub in range(2):
-            at = [[cv[s, p, sub, band] for p in range(2)] for s in range(SLOTS)]
-            add_products(sums, masked(rim_lanes, at), rights_of(at))
-        for p, n, m in each_sum():
-            value = acc[p, n, m, band, :] + sums[p][n][m]
-            acc[p, n, m, band, :] = value * SIXTH if m == 1 else value
-
-    count = 2 * MOMENTS * MOMENTS * rows
-    rest = acc[...].reshape(count, LANES)
-    ones = jnp.ones((SUBS, LANES), jnp.bfloat16)
-    total = None
-    for _ in range(3):
-        piece = rest.astype(jnp.bfloat16)
-        rest = rest - piece.astype(jnp.float32)
-        part = lax.dot_general(
-            ones, piece, (((1,), (1,)), ((), ())), preferred_element_type=jnp.float32
-        )
-        total = part if total is None else total + part
-
     row8 = jnp.where(sub8 < 4, jnp.where(sub8 == 2, 1, 0), jnp.where(sub8 == 6, rows - 2, rows - 1))
     row8 = jnp.where((sub8 == 0) | (sub8 == 4), -LANES, row8)
     per = LANES // rows
@@ -628,9 +649,11 @@
                 pltpu.VMEM((4, 7, rows, cols), f32),
                 pltpu.VMEM((4, 7, SUBS, cols), f32),
                 pltpu.VMEM((5, SUBS, LANES), f32),
+                pltpu.VMEM((2, SUBS, LANES), f32),
+                pltpu.VMEM((2, rows, LANES), f32),
                 pltpu.VMEM((5, tall, LANES), f32),
-                pltpu.VMEM((5, tall, LANES), f32),
-                pltpu.VMEM((5, tall, LANES), f32),
+                pltpu.VMEM((2, tall, LANES), f32),
+                pltpu.VMEM((2, tall, LANES), f32),
                 pltpu.VMEM((7, tall, LANES), f32),
                 pltpu.VMEM((SLOTS, 2, 2, rows, LANES), f32),
                 pltpu.VMEM((count, 2, SLOTS, SUBS, cols), f32),

time: 15.7 us -> 15.5 us (0.987)
  Pallas kernels: 14.9 us -> 14.7 us
    pallas_call x1, Pallas kernels: 14.1 us -> 13.9 us  [per_device(): pl.pallas_call(functools.partial(kernel, gxn, gyn), out_shape=(pltpu.VMEM...]
where the time goes in v4:
time: 15.5 us; the launch traced here: 15.3 us
  Pallas kernels  14.7 us (95%)
  between operations  0.64 us (4%)
    pallas_call x1, Pallas kernels, per_device(): pl.pallas_call(functools.partial(kernel, gxn, gyn), out_shape=(pltpu.VMEM...  13.9 us
    pallas_call x1, Pallas kernels, per_device(): pl.pallas_call(writer, out_shape=(jax.ShapeDtypeStruct((MOMENTS, MOMENTS,...  0.82 us

profile of v4, /device:TPU:0, one launch (start us, length us, event | category | flops | bytes accessed | tf_op | source)
XLA Modules:
  0.0 15.3 jit_solution(3405904742641284248)
XLA Ops:
  0.6 13.9 %shard_map.58 = (f32[8,288]{1,0:T(8,128)S(1)}, bf16[8,2,2,16,256]{4,3,2,1,0:T(8,128)(2,1)S(1)}, bf16[8,2,2,16,256]{4,3,2,1,0:T(8,128)(2,1)S(1)}) custom-call(f32[8,2,2,16,256]{4,3,2,1,0:T(8,128)} %vec.1, f32[3,16,256]{2,1,0:T(8,128)} %bonds.1, f32[2,16,256]{2,1,0:T(8,128)} %onsite.1), custom_call_target="tpu_custom_call" | custom-call | tf_op jit(solution)/shard_map/pallas_call | solution.py:633
  14.5 0.8 %shard_map.59 = (f32[3,3,2,16]{3,2,1,0:T(2,128)}, bf16[8,2,2,16,256]{4,3,2,1,0:T(8,128)(2,1)}, bf16[8,2,2,16,256]{4,3,2,1,0:T(8,128)(2,1)}) custom-call(f32[8,288]{1,0:T(8,128)S(1)} %get-tuple-element.9.total, bf16[8,2,2,16,256]{4,3,2,1,0:T(8,128)(2,1)S(1)} %get-tuple-element.10.lbuf, bf16[8,2,2,16,256]{4,3,2,1,0:T(8,128)(2,1)S(1)} %get-tuple-element.11.rbuf), custom_call_target="tpu_custom_call" | custom-call | tf_op jit(solution)/shard_map/pallas_call | solution.py:676

commit v5 on v4

--- a/solution.py
+++ b/solution.py
@@ -589,14 +589,14 @@
 
     lax.fori_loop(0, vectors, patch, 0)
 
+    for copy in sends + swaps:
+        copy.wait_send()
     for copy in swaps:
         copy.wait_recv()
     total = part_mom[0]
     for d in range(1, gyn):
         total = total + part_mom[d]
     out_mom[...] = total / float(vectors * cols * gyn)
-    for copy in sends + swaps:
-        copy.wait_send()
 
 
 def writer(total, lbuf, rbuf, out_mom, out_left, out_right, mom, out_sem):

time: 15.5 us -> 15.4 us (level)
  no operation moved by 1% of the time
where the time goes in v5:
time: 15.4 us; the launch traced here: 15.3 us
  Pallas kernels  14.6 us (95%)
  between operations  0.64 us (4%)
    pallas_call x1, Pallas kernels, per_device(): pl.pallas_call(functools.partial(kernel, gxn, gyn), out_shape=(pltpu.VMEM...  13.8 us
    pallas_call x1, Pallas kernels, per_device(): pl.pallas_call(writer, out_shape=(jax.ShapeDtypeStruct((MOMENTS, MOMENTS,...  0.82 us

profile of v5, /device:TPU:0, one launch (start us, length us, event | category | flops | bytes accessed | tf_op | source)
XLA Modules:
  0.0 15.3 jit_solution(13331858270824051980)
XLA Ops:
  0.6 13.8 %shard_map.58 = (f32[8,288]{1,0:T(8,128)S(1)}, bf16[8,2,2,16,256]{4,3,2,1,0:T(8,128)(2,1)S(1)}, bf16[8,2,2,16,256]{4,3,2,1,0:T(8,128)(2,1)S(1)}) custom-call(f32[8,2,2,16,256]{4,3,2,1,0:T(8,128)} %vec.1, f32[3,16,256]{2,1,0:T(8,128)} %bonds.1, f32[2,16,256]{2,1,0:T(8,128)} %onsite.1), custom_call_target="tpu_custom_call" | custom-call | tf_op jit(solution)/shard_map/pallas_call | solution.py:633
  14.5 0.8 %shard_map.59 = (f32[3,3,2,16]{3,2,1,0:T(2,128)}, bf16[8,2,2,16,256]{4,3,2,1,0:T(8,128)(2,1)}, bf16[8,2,2,16,256]{4,3,2,1,0:T(8,128)(2,1)}) custom-call(f32[8,288]{1,0:T(8,128)S(1)} %get-tuple-element.9.total, bf16[8,2,2,16,256]{4,3,2,1,0:T(8,128)(2,1)S(1)} %get-tuple-element.10.lbuf, bf16[8,2,2,16,256]{4,3,2,1,0:T(8,128)(2,1)S(1)} %get-tuple-element.11.rbuf), custom_call_target="tpu_custom_call" | custom-call | tf_op jit(solution)/shard_map/pallas_call | solution.py:676
